TPU v7x, 32 devices: a whole 2x2x4 slice. The times are simulated.
32 devices in a mesh: groups: 2 (over x), space: 16 (over z, y, core).
Axes of the slice: x: 2, y: 2, z: 4, core: 2. Of those that a mesh axis runs over, the one named last changes fastest.
Arguments:
- inputs: bfloat16 [768, 1152, 256], P(('groups', 'space')), parts along dimension 0, may hold values from -6 to 6
- spectral_weight: bfloat16 [2, 256, 2, 256, 256], P(None, 'space'), may hold values from -0.25 to 0.25
- local_weight: bfloat16 [2, 256, 256], replicated, may hold values from -0.375 to 0.375
- layer_bias: bfloat16 [2, 256], replicated, may hold values from -3 to 3
- readout_hidden: bfloat16 [256, 256], replicated, may hold values from -0.375 to 0.375
- readout_final: bfloat16 [20, 256], replicated, may hold values from -0.375 to 0.375
Outputs:
- forecast: bfloat16 [20, 768, 1152], P(None, ('groups', 'space')), parts along dimension 1
There are 2 independent parts, one for each index of `groups`. A program takes and returns all parts, laid end to end along the dimension named above; an argument that names none is the same for every part. Nothing has to cross between parts.
All inputs are finite; a program needn't handle non-finite values.
Results may differ from a plain program's by a relative error of at most 0.018.
Values may be sent and summed in bfloat16 or wider, within the bound.
A program may use at most 128 MiB of HBM per device.

v0:
```python
import jax
import jax.numpy as jnp
from jax import lax
from jax.sharding import PartitionSpec as P

KY = 16
KX = 16
LAYERS = 2
MODES = 256


def zonal_tables(columns, modes):
    column_ids = jnp.arange(columns, dtype=jnp.int32)
    wave_numbers = jnp.arange(1, modes + 1, dtype=jnp.int32)
    phase_int = column_ids[:, None] * wave_numbers[None, :] % columns
    angles = 2.0 * jnp.pi / columns * phase_int.astype(jnp.float32)
    cosines = jnp.cos(angles)
    sines = jnp.sin(angles)
    forward = jnp.concatenate([cosines, -sines], axis=1) / jnp.sqrt(jnp.float32(columns))
    inverse = jnp.stack([cosines, -sines], axis=2).reshape(columns, 2 * modes) * jnp.sqrt(
        jnp.float32(2.0 / modes)
    )
    return (forward.astype(jnp.bfloat16), inverse.astype(jnp.bfloat16))


def meridional_tables(row_ids, height, modes):
    mode_index = jnp.arange(modes, dtype=jnp.int32)
    wave_numbers = jnp.where(mode_index < modes // 2, mode_index, mode_index - modes)
    phase_int = wave_numbers[:, None] * row_ids[None, :] % height
    angles = 2.0 * jnp.pi / height * phase_int.astype(jnp.float32)
    cosines = jnp.cos(angles)
    sines = jnp.sin(angles)
    forward = jnp.stack(
        [jnp.stack([cosines, sines], axis=2), jnp.stack([-sines, cosines], axis=2)], axis=1
    )
    forward = forward / jnp.sqrt(jnp.float32(height))
    cos_rows = cosines.T
    sin_rows = sines.T
    inverse = jnp.stack(
        [jnp.stack([cos_rows, -sin_rows], axis=2), jnp.stack([sin_rows, cos_rows], axis=2)], axis=1
    )
    inverse = inverse / jnp.sqrt(jnp.float32(modes))
    return (forward.astype(jnp.bfloat16), inverse.astype(jnp.bfloat16))


def mix_modes(spectrum, weights):
    real_in = spectrum[:, 0]
    imag_in = spectrum[:, 1]
    real_weight = weights[:, 0]
    imag_weight = weights[:, 1]

    def product(vectors, matrices):
        return jnp.einsum("mi,mio->mo", vectors, matrices, preferred_element_type=jnp.float32)

    real_out = product(real_in, real_weight) - product(imag_in, imag_weight)
    imag_out = product(real_in, imag_weight) + product(imag_in, real_weight)
    return jnp.stack([real_out, imag_out], axis=1).astype(jnp.bfloat16)


def per_device(inputs, spectral_weight, local_weight, layer_bias, readout_hidden, readout_final):
    rows_here, columns, channels = inputs.shape
    devices_along = lax.axis_size("space")
    height = rows_here * devices_along
    zonal_forward, zonal_inverse = zonal_tables(columns, KX)
    local_rows = jnp.arange(rows_here, dtype=jnp.int32) * devices_along + lax.axis_index("space")
    forward_here, inverse_here = meridional_tables(local_rows, height, KY)
    current = inputs
    for layer_index in range(LAYERS):
        zonal_part = jnp.einsum(
            "hwc,wj->hjc", current, zonal_forward, preferred_element_type=jnp.float32
        )
        zonal_view = zonal_part.astype(jnp.bfloat16).reshape(rows_here, 2, KX, channels)
        partial_value = jnp.einsum(
            "qphr,hrkc->qkpc", forward_here, zonal_view, preferred_element_type=jnp.float32
        )
        partial_value = partial_value.reshape(MODES, 2 * channels)
        spectrum = lax.psum_scatter(
            partial_value, "space", scatter_dimension=0, tiled=True
        ).reshape(-1, 2, channels)
        mixed = mix_modes(spectrum.astype(jnp.bfloat16), spectral_weight[layer_index])
        all_modes = lax.all_gather(mixed, "space", axis=0, tiled=True).reshape(KY, KX, 2, channels)
        returned = jnp.einsum(
            "hpqr,qkrc->hkpc", inverse_here, all_modes, preferred_element_type=jnp.float32
        )
        returned = returned.astype(jnp.bfloat16).reshape(rows_here, 2 * KX, channels)
        spread = jnp.einsum(
            "wj,hjc->hwc", zonal_inverse, returned, preferred_element_type=jnp.float32
        )
        pointwise = jnp.dot(
            current.reshape(-1, channels),
            local_weight[layer_index],
            preferred_element_type=jnp.float32,
        )
        pointwise = pointwise.reshape(current.shape)
        bias_now = layer_bias[layer_index].astype(jnp.float32)
        current = jax.nn.gelu(spread + pointwise + bias_now, approximate=True).astype(jnp.bfloat16)
    hidden = jnp.dot(
        current.reshape(-1, channels), readout_hidden, preferred_element_type=jnp.float32
    )
    hidden = jax.nn.gelu(hidden, approximate=True).astype(jnp.bfloat16)
    final = jnp.einsum("pq,nq->pn", readout_final, hidden, preferred_element_type=jnp.float32)
    return final.astype(jnp.bfloat16).reshape(readout_final.shape[0], rows_here, columns)


def solution(mesh):
    in_specs = (
        P(("groups", "space"), None, None),
        P(None, "space", None, None, None),
        P(),
        P(),
        P(),
        P(),
    )
    out_specs = P(None, ("groups", "space"), None)
    return jax.shard_map(
        per_device, mesh=mesh, in_specs=in_specs, out_specs=out_specs, check_vma=False
    )
```

profile of v0, /device:TPU:0, one launch (start us, length us, event | category | flops | bytes accessed | tf_op | source)
XLA Modules:
  0.0 308.6 jit_solution(3359486465415475526)
XLA Ops:
  6.5 0.0 copy-start
  6.5 0.0 copy-start.1
  6.5 0.0 reduce-scatter.3.cloned.1.call-start
  6.6 0.4 fusion.64
  7.0 0.1 fusion.101
  7.1 7.5 %convolution_convert_fusion.2 = bf16[32,24,256]{2,0,1:T(8,128)(2,1)S(1)} fusion(bf16[24,1152,256]{2,1,0:T(8,128)(2,1)} %param.6, f32[1152,16]{0,1:T(8,128)S(1)} %get-tuple-element.26, f32[1152,16]{0,1:T(8,128)S(1)} %get-tuple-element.25), kind=kOutput, calls=%fused_computation.49 | convolution fusion | flops 453292032 | bytes 14696448 | tf_op jit(solution)/shard_map/hwc,wj->hjc/dot_general | solution.py:69
  14.6 0.4 convolution_bitcast_fusion.3
  15.0 0.4 copy.42
  15.4 0.8 copy.96
  16.3 0.0 reduce-scatter.3.cloned.1.call-update
  16.3 0.0 reduce-scatter.5.cloned.1.call-start
  16.3 0.1 fusion.110
  16.5 0.4 fusion.61
  16.9 0.0 copy-done.1
  16.9 6.0 %slice_bitcast_fusion.1 = (bf16[16,2,256,256]{3,2,1,0:T(8,128)(2,1)}, bf16[16,2,256,256]{3,2,1,0:T(8,128)(2,1)}) fusion(bf16[2,16,2,256,256]{4,3,2,1,0:T(8,128)(2,1)} %param.7), kind=kLoop, calls=%fused_computation.33 | loop fusion | bytes 16777216 | tf_op jit(solution)/shard_map/squeeze | solution.py:80
  22.8 52.5 %reduce-scatter.3.cloned.1.call-done = f32[16,512]{1,0:T(8,128)} async-done(((f32[256,512]{1,0:T(8,128)}), f32[16,512]{1,0:T(8,128)}) %reduce-scatter.3.cloned.1.call-update) | async-done | bytes 32784 | tf_op jit(solution)/shard_map/reduce_scatter | solution.py:77
  75.3 0.8 convert_element_type.150
  76.1 2.0 fusion.29
  78.1 2.0 fusion.28
  80.1 2.0 fusion.27
  82.1 2.0 fusion.30
  84.1 20.3 %all_gather.6 = bf16[256,2,256]{2,0,1:T(8,128)(2,1)S(1)} all-gather(bf16[16,2,256]{2,0,1:T(8,128)(2,1)S(1)} %pad_maximum_fusion), channel_id=1, replica_groups=mesh['groups'=2,'space'=16] {'space'}, dimensions={0}, use_global_device_ids=true | all-gather | bytes 278528 | tf_op jit(solution)/shard_map/all_gather | solution.py:81
  104.4 0.3 fusion.38
  104.7 0.0 copy-start.2
  104.7 11.4 %fusion.43 = f32[24,256,1152,1]{2,1,3,0:T(8,128)} fusion(bf16[24,16,2,256]{3,0,2,1:T(8,128)(2,1)S(1)} %fusion.38, f32[1152,16,1]{0,1,2:T(8,128)S(1)} %get-tuple-element.24, f32[1152,16,1]{0,1,2:T(8,128)S(1)} %get-tuple-element.23), kind=kOutput, calls=%fused_computation.60 | convolution fusion | flops 453095424 | bytes 28852224 | tf_op jit(solution)/shard_map/wj,hjc->hwc/dot_general | solution.py:86
  116.1 0.0 copy-done.2
  116.1 24.0 %fusion.7 = bf16[24,1152,256]{1,2,0:T(8,128)(2,1)} fusion(f32[24,256,1152,1]{2,1,3,0:T(8,128)} %fusion.43, bf16[24,1152,256]{2,1,0:T(8,128)(2,1)} %param.6, f32[256]{0:T(256)S(1)} %bitcast.212, bf16[2,256,256]{2,1,0:T(8,128)(2,1)S(1)} %copy-done.2), kind=kOutput, calls=%fused_computation.11 | convolution fusion | flops 3701735424 | bytes 56755200 | tf_op jit(solution)/shard_map/dot_general | solution.py:89
  140.1 9.3 %convolution_convert_fusion.1 = bf16[32,24,256]{2,0,1:T(8,128)(2,1)S(1)} fusion(bf16[24,1152,256]{1,2,0:T(8,128)(2,1)} %fusion.7, f32[1152,16]{0,1:T(8,128)S(1)} %get-tuple-element.26, f32[1152,16]{0,1:T(8,128)S(1)} %get-tuple-element.25), kind=kOutput, calls=%fused_computation.48 | convolution fusion | flops 453292032 | bytes 14696448 | tf_op jit(solution)/shard_map/hwc,wj->hjc/dot_general | solution.py:69
  149.4 0.3 convolution_bitcast_fusion.2
  149.8 0.4 copy.50
  150.2 0.8 copy.97
  151.0 0.0 reduce-scatter.5.cloned.1.call-update
  151.0 53.6 %reduce-scatter.5.cloned.1.call-done = f32[16,512]{1,0:T(8,128)} async-done(((f32[256,512]{1,0:T(8,128)}), f32[16,512]{1,0:T(8,128)}) %reduce-scatter.5.cloned.1.call-update) | async-done | bytes 32784 | tf_op jit(solution)/shard_map/reduce_scatter | solution.py:77
  204.6 0.8 convert_element_type.163
  205.4 2.0 fusion.31
  207.4 2.0 fusion.34
  209.4 2.0 fusion.33
  211.3 2.0 fusion.32
  213.4 20.3 %all_gather.7 = bf16[256,2,256]{2,0,1:T(8,128)(2,1)S(1)} all-gather(bf16[16,2,256]{2,0,1:T(8,128)(2,1)S(1)} %pad_maximum_fusion.1), channel_id=1, replica_groups=mesh['groups'=2,'space'=16] {'space'}, dimensions={0}, use_global_device_ids=true | all-gather | bytes 278528 | tf_op jit(solution)/shard_map/all_gather | solution.py:81
  233.7 0.3 fusion.37
  234.0 11.4 %fusion.41 = f32[24,256,1152,1]{2,1,3,0:T(8,128)} fusion(bf16[24,16,2,256]{3,0,2,1:T(8,128)(2,1)S(1)} %fusion.37, f32[1152,16,1]{0,1,2:T(8,128)S(1)} %get-tuple-element.24, f32[1152,16,1]{0,1,2:T(8,128)S(1)} %get-tuple-element.23), kind=kOutput, calls=%fused_computation.58 | convolution fusion | flops 453095424 | bytes 28852224 | tf_op jit(solution)/shard_map/wj,hjc->hwc/dot_general | solution.py:86
  245.4 24.4 %fusion.15 = bf16[24,1152,256]{1,2,0:T(8,128)(2,1)} fusion(f32[24,256,1152,1]{2,1,3,0:T(8,128)} %fusion.41, bf16[24,1152,256]{1,2,0:T(8,128)(2,1)} %fusion.7, f32[256]{0:T(256)S(1)} %bitcast.211, bf16[2,256,256]{2,1,0:T(8,128)(2,1)S(1)} %copy-done.2), kind=kOutput, calls=%fused_computation.19 | convolution fusion | flops 3701735424 | bytes 56755200 | tf_op jit(solution)/shard_map/dot_general | solution.py:89
  269.8 18.7 %copy.57 = bf16[24,1152,256]{2,1,0:T(8,128)(2,1)} copy(bf16[24,1152,256]{1,2,0:T(8,128)(2,1)} %fusion.15) | data formatting | bytes 28311552 | tf_op jit(solution)/shard_map/convert_element_type | solution.py:96
  288.5 0.0 copy-done
  288.5 0.0 copy-done.3
  288.5 12.0 %convolution_convert_fusion = bf16[27648,20]{0,1:T(8,128)(2,1)S(1)} fusion(bf16[20,256]{1,0:T(8,128)(2,1)S(1)} %copy-done.3, bf16[27648,256]{1,0:T(8,128)(2,1)} %bitcast.196, bf16[256,256]{1,0:T(8,128)(2,1)S(1)} %copy-done), kind=kOutput, calls=%fused_computation.3 | convolution fusion | flops 3971248128 | bytes 15403008 | tf_op jit(solution)/shard_map/pq,nq->pn/dot_general | solution.py:101
  300.5 0.2 copy.98
  300.6 1.1 slice.64
  (20 shorter events, 0.2 us)
Async XLA Ops:
  6.5 282.0 %copy-start = (bf16[256,256]{1,0:T(8,128)(2,1)S(1)}, bf16[256,256]{1,0:T(8,128)(2,1)}, u32[]{:S(2)}) copy-start(bf16[256,256]{1,0:T(8,128)(2,1)} %param.10) | copy-start | bytes 393220
  6.5 10.3 %copy-start.1 = (bf16[2,256]{1,0:T(2,128)(2,1)S(1)}, bf16[2,256]{1,0:T(2,128)(2,1)}, u32[]{:S(2)}) copy-start(bf16[2,256]{1,0:T(2,128)(2,1)} %param.9) | copy-start | bytes 3076
  6.5 68.8 %reduce-scatter.3.cloned.1.call-start = ((), (), s32[]{:S(2)}) async-start(), calls=%async_computation.2 | async-start | bytes 557056 | tf_op jit(solution)/shard_map/reduce_scatter | solution.py:77
  16.3 188.3 %reduce-scatter.5.cloned.1.call-start = ((), (), s32[]{:S(2)}) async-start(), calls=%async_computation.3 | async-start | bytes 557056 | tf_op jit(solution)/shard_map/reduce_scatter | solution.py:77
  104.7 11.4 %copy-start.2 = (bf16[2,256,256]{2,1,0:T(8,128)(2,1)S(1)}, bf16[2,256,256]{2,1,0:T(8,128)(2,1)}, u32[]{:S(2)}) copy-start(bf16[2,256,256]{2,1,0:T(8,128)(2,1)} %param.8) | copy-start | bytes 786436
  269.8 18.7 %copy-start.3 = (bf16[20,256]{1,0:T(8,128)(2,1)S(1)}, bf16[20,256]{1,0:T(8,128)(2,1)}, u32[]{:S(2)}) copy-start(bf16[20,256]{1,0:T(8,128)(2,1)} %param.11) | copy-start | bytes 30724
Sparse Core Ops, SparseCore 0:
  16.4 58.8 reduce-scatter.2
  151.1 53.3 reduce-scatter.4
where the time goes:
time: 310 us; the launch traced here: 309 us
  matrix products  117 us (38%)
  waiting for transfers between devices  106 us (34%)
  blocking collectives  40.7 us (13%)
  local copies, waits for them, and re-layouts  28.5 us (9%)
  between operations  13.6 us (4%)
    reduce_scatter x2, waiting for transfers between devices, per_device(): lax.psum_scatter(partial_value, 'space', scatter_dimension=0, tiled=True)  106 us
    dot_general x2, matrix products, per_device(): jnp.dot(current.reshape(-1, channels), local_weight[layer_index], preferr...  48.4 us
    all_gather x2, blocking collectives, per_device(): lax.all_gather(mixed, 'space', axis=0, tiled=True)  40.7 us
    dot_general x2, matrix products, per_device(): jnp.einsum('wj,hjc->hwc', zonal_inverse, returned, preferred_element_type...  22.8 us
    convert_element_type x1, local copies, waits for them, and re-layouts, per_device(): jax.nn.gelu(spread + pointwise + bias_now, approximate=True)  18.7 us
    dot_general x2, matrix products, per_device(): jnp.einsum('hwc,wj->hjc', current, zonal_forward, preferred_element_type=...  16.8 us
    dot_general x8, matrix products, product(): jnp.einsum('mi,mio->mo', vectors, matrices, preferred_element_type=jnp.fl...  15.8 us
    dot_general x1, matrix products, per_device(): jnp.einsum('pq,nq->pn', readout_final, hidden, preferred_element_type=jnp...  12 us
  transfers between devices with their start and end apart: 2, of which 2 were waited for; matrix products, arithmetic and copies ran while one was open for 2% of the time, Pallas kernels for 0%

commit v1 on v0

--- a/solution.py
+++ b/solution.py
@@ -78,7 +78,9 @@
             partial_value, "space", scatter_dimension=0, tiled=True
         ).reshape(-1, 2, channels)
         mixed = mix_modes(spectrum.astype(jnp.bfloat16), spectral_weight[layer_index])
-        all_modes = lax.all_gather(mixed, "space", axis=0, tiled=True).reshape(KY, KX, 2, channels)
+        all_modes = jnp.concatenate(
+            lax.all_to_all(jnp.stack([mixed] * lax.axis_size("space")), "space", 0, 0), axis=0
+        ).reshape(KY, KX, 2, channels)
         returned = jnp.einsum(
             "hpqr,qkrc->hkpc", inverse_here, all_modes, preferred_element_type=jnp.float32
         )

time: 310 us -> 298 us (0.961)
  blocking collectives: 40.7 us -> 13.5 us
  waiting for transfers between devices: 106 us -> 117 us
  starting transfers between devices: 0.04 us -> 3.97 us
    all_gather x2 -> x0, blocking collectives: 40.7 us -> none  [per_device(): lax.all_gather(mixed, 'space', axis=0, tiled=True)]
    all_to_all x0 -> x1, blocking collectives: none -> 13.5 us  [per_device(): lax.all_to_all(jnp.stack([mixed] * lax.axis_size('space')), 'space', 0, 0)]
    all_to_all x0 -> x1, waiting for transfers between devices: none -> 9.38 us  [per_device(): lax.all_to_all(jnp.stack([mixed] * lax.axis_size('space')), 'space', 0, 0)]
    all_to_all x0 -> x1, starting transfers between devices: none -> 3.75 us  [per_device(): lax.all_to_all(jnp.stack([mixed] * lax.axis_size('space')), 'space', 0, 0)]
  transfers between devices with their start and end apart: 2 -> 3, of which waited for: 2 -> 3; matrix products, arithmetic and copies ran while one was open for 2% -> 2% of each run, Pallas kernels for 0% -> 0%
where the time goes in v1:
time: 298 us; the launch traced here: 297 us
  matrix products  117 us (39%)
  waiting for transfers between devices  117 us (39%)
  local copies, waits for them, and re-layouts  29.6 us (10%)
  between operations  13.6 us (5%)
  blocking collectives  13.5 us (5%)
  starting transfers between devices  3.97 us (1%)
    reduce_scatter x2, waiting for transfers between devices, per_device(): lax.psum_scatter(partial_value, 'space', scatter_dimension=0, tiled=True)  107 us
    dot_general x2, matrix products, per_device(): jnp.dot(current.reshape(-1, channels), local_weight[layer_index], preferr...  48.4 us
    dot_general x2, matrix products, per_device(): jnp.einsum('wj,hjc->hwc', zonal_inverse, returned, preferred_element_type...  22.8 us
    convert_element_type x1, local copies, waits for them, and re-layouts, per_device(): jax.nn.gelu(spread + pointwise + bias_now, approximate=True)  18.7 us
    dot_general x2, matrix products, per_device(): jnp.einsum('hwc,wj->hjc', current, zonal_forward, preferred_element_type=...  16.8 us
    dot_general x8, matrix products, product(): jnp.einsum('mi,mio->mo', vectors, matrices, preferred_element_type=jnp.fl...  15.8 us
    all_to_all x1, blocking collectives, per_device(): lax.all_to_all(jnp.stack([mixed] * lax.axis_size('space')), 'space', 0, 0)  13.5 us
    dot_general x1, matrix products, per_device(): jnp.einsum('pq,nq->pn', readout_final, hidden, preferred_element_type=jnp...  12 us
  transfers between devices with their start and end apart: 3, of which 3 were waited for; matrix products, arithmetic and copies ran while one was open for 2% of the time, Pallas kernels for 0%

profile of v1, /device:TPU:0, one launch (start us, length us, event | category | flops | bytes accessed | tf_op | source)
XLA Modules:
  0.0 297.3 jit_solution(11426819132431933586)
XLA Ops:
  6.5 0.0 copy-start
  6.5 0.0 reduce-scatter.3.cloned.1.call-start
  6.6 0.4 fusion.64
  7.0 0.1 fusion.101
  7.1 7.5 %convolution_convert_fusion.2 = bf16[32,24,256]{2,0,1:T(8,128)(2,1)S(1)} fusion(bf16[24,1152,256]{2,1,0:T(8,128)(2,1)} %param.6, f32[1152,16]{0,1:T(8,128)S(1)} %get-tuple-element.26, f32[1152,16]{0,1:T(8,128)S(1)} %get-tuple-element.25), kind=kOutput, calls=%fused_computation.49 | convolution fusion | flops 453292032 | bytes 14696448 | tf_op jit(solution)/shard_map/hwc,wj->hjc/dot_general | solution.py:69
  14.6 0.4 convolution_bitcast_fusion.3
  15.0 0.4 copy.63
  15.4 0.8 copy.119
  16.3 0.0 reduce-scatter.3.cloned.1.call-update
  16.3 0.0 copy-done.1
  16.3 0.1 fusion.110
  16.4 6.0 %slice_bitcast_fusion.1 = (bf16[16,2,256,256]{3,2,1,0:T(8,128)(2,1)}, bf16[16,2,256,256]{3,2,1,0:T(8,128)(2,1)}) fusion(bf16[2,16,2,256,256]{4,3,2,1,0:T(8,128)(2,1)} %param.7), kind=kLoop, calls=%fused_computation.33 | loop fusion | bytes 16777216 | tf_op jit(solution)/shard_map/squeeze | solution.py:80
  22.4 52.9 %reduce-scatter.3.cloned.1.call-done = f32[16,512]{1,0:T(8,128)} async-done(((f32[256,512]{1,0:T(8,128)}), f32[16,512]{1,0:T(8,128)}) %reduce-scatter.3.cloned.1.call-update) | async-done | bytes 32784 | tf_op jit(solution)/shard_map/reduce_scatter | solution.py:77
  75.3 0.8 convert_element_type.154
  76.1 2.0 fusion.29
  78.1 2.0 fusion.28
  80.1 2.0 fusion.27
  82.1 2.0 fusion.30
  84.1 0.9 stack.46
  85.0 3.7 %all-to-all-start = ((bf16[16,16,2,256]{3,2,1,0:T(2,128)(2,1)}), bf16[16,16,2,256]{3,2,1,0:T(2,128)(2,1)S(1)}, u32[]{:S(2)}, u32[]{:S(2)}) async-start(bf16[16,16,2,256]{3,2,1,0:T(2,128)(2,1)} %stack.46), calls=%async_computation.1 | async-start | bytes 524288 | tf_op jit(solution)/shard_map/all_to_all | solution.py:82
  88.8 0.2 reduce-scatter.5.cloned.1.call-start
  89.0 0.4 fusion.61
  89.4 9.4 %all-to-all-done = bf16[16,16,2,256]{3,2,1,0:T(2,128)(2,1)S(1)} async-done(((bf16[16,16,2,256]{3,2,1,0:T(2,128)(2,1)}), bf16[16,16,2,256]{3,2,1,0:T(2,128)(2,1)S(1)}, u32[]{:S(2)}, u32[]{:S(2)}) %all-to-all-start) | async-done | bytes 262176 | tf_op jit(solution)/shard_map/all_to_all | solution.py:82
  98.8 0.3 fusion.38
  99.1 0.0 copy-start.2
  99.1 11.4 %fusion.43 = f32[24,256,1152,1]{2,1,3,0:T(8,128)} fusion(bf16[24,16,2,256]{3,0,2,1:T(8,128)(2,1)S(1)} %fusion.38, f32[1152,16,1]{0,1,2:T(8,128)S(1)} %get-tuple-element.24, f32[1152,16,1]{0,1,2:T(8,128)S(1)} %get-tuple-element.23), kind=kOutput, calls=%fused_computation.60 | convolution fusion | flops 453095424 | bytes 28852224 | tf_op jit(solution)/shard_map/wj,hjc->hwc/dot_general | solution.py:88
  110.5 0.0 copy-done.2
  110.5 24.0 %fusion.7 = bf16[24,1152,256]{1,2,0:T(8,128)(2,1)} fusion(f32[24,256,1152,1]{2,1,3,0:T(8,128)} %fusion.43, bf16[24,1152,256]{2,1,0:T(8,128)(2,1)} %param.6, f32[256]{0:T(256)S(1)} %bitcast.208, bf16[2,256,256]{2,1,0:T(8,128)(2,1)S(1)} %copy-done.2), kind=kOutput, calls=%fused_computation.11 | convolution fusion | flops 3701735424 | bytes 56755200 | tf_op jit(solution)/shard_map/dot_general | solution.py:91
  134.5 9.2 %convolution_convert_fusion.1 = bf16[32,24,256]{2,0,1:T(8,128)(2,1)S(1)} fusion(bf16[24,1152,256]{1,2,0:T(8,128)(2,1)} %fusion.7, f32[1152,16]{0,1:T(8,128)S(1)} %get-tuple-element.26, f32[1152,16]{0,1:T(8,128)S(1)} %get-tuple-element.25), kind=kOutput, calls=%fused_computation.48 | convolution fusion | flops 453292032 | bytes 14696448 | tf_op jit(solution)/shard_map/hwc,wj->hjc/dot_general | solution.py:69
  143.8 0.4 convolution_bitcast_fusion.2
  144.1 0.4 copy.72
  144.5 0.8 copy.120
  145.4 0.0 reduce-scatter.5.cloned.1.call-update
  145.4 54.5 %reduce-scatter.5.cloned.1.call-done = f32[16,512]{1,0:T(8,128)} async-done(((f32[256,512]{1,0:T(8,128)}), f32[16,512]{1,0:T(8,128)}) %reduce-scatter.5.cloned.1.call-update) | async-done | bytes 32784 | tf_op jit(solution)/shard_map/reduce_scatter | solution.py:77
  199.9 0.8 convert_element_type.167
  200.7 2.0 fusion.31
  202.7 2.0 fusion.34
  204.7 2.0 fusion.33
  206.6 2.0 fusion.32
  208.7 0.2 stack.56
  208.9 13.5 %all_to_all.10 = bf16[16,16,2,256]{3,2,1,0:T(2,128)(2,1)S(1)} all-to-all(bf16[16,16,2,256]{3,2,1,0:T(2,128)(2,1)S(1)} %stack.56), channel_id=1, replica_groups=mesh['groups'=2,'space'=16] {'space'}, dimensions={0} | all-to-all | bytes 524288 | tf_op jit(solution)/shard_map/all_to_all | solution.py:82
  222.4 0.3 fusion.37
  222.7 11.4 %fusion.41 = f32[24,256,1152,1]{2,1,3,0:T(8,128)} fusion(bf16[24,16,2,256]{3,0,2,1:T(8,128)(2,1)S(1)} %fusion.37, f32[1152,16,1]{0,1,2:T(8,128)S(1)} %get-tuple-element.24, f32[1152,16,1]{0,1,2:T(8,128)S(1)} %get-tuple-element.23), kind=kOutput, calls=%fused_computation.58 | convolution fusion | flops 453095424 | bytes 28852224 | tf_op jit(solution)/shard_map/wj,hjc->hwc/dot_general | solution.py:88
  234.1 24.4 %fusion.15 = bf16[24,1152,256]{1,2,0:T(8,128)(2,1)} fusion(f32[24,256,1152,1]{2,1,3,0:T(8,128)} %fusion.41, bf16[24,1152,256]{1,2,0:T(8,128)(2,1)} %fusion.7, f32[256]{0:T(256)S(1)} %bitcast.207, bf16[2,256,256]{2,1,0:T(8,128)(2,1)S(1)} %copy-done.2), kind=kOutput, calls=%fused_computation.19 | convolution fusion | flops 3701735424 | bytes 56755200 | tf_op jit(solution)/shard_map/dot_general | solution.py:91
  258.6 18.7 %copy.80 = bf16[24,1152,256]{2,1,0:T(8,128)(2,1)} copy(bf16[24,1152,256]{1,2,0:T(8,128)(2,1)} %fusion.15) | data formatting | bytes 28311552 | tf_op jit(solution)/shard_map/convert_element_type | solution.py:98
  277.2 12.0 %convolution_convert_fusion = bf16[27648,20]{0,1:T(8,128)(2,1)S(1)} fusion(bf16[20,256]{1,0:T(8,128)(2,1)S(1)} %copy-done.3, bf16[27648,256]{1,0:T(8,128)(2,1)} %bitcast.192, bf16[256,256]{1,0:T(8,128)(2,1)S(1)} %copy-done), kind=kOutput, calls=%fused_computation.3 | convolution fusion | flops 3971248128 | bytes 15403008 | tf_op jit(solution)/shard_map/pq,nq->pn/dot_general | solution.py:103
  289.2 0.2 copy.121
  289.4 1.1 slice.64
  (25 shorter events, 0.2 us)
Async XLA Ops:
  6.5 270.7 %copy-start = (bf16[256,256]{1,0:T(8,128)(2,1)S(1)}, bf16[256,256]{1,0:T(8,128)(2,1)}, u32[]{:S(2)}) copy-start(bf16[256,256]{1,0:T(8,128)(2,1)} %param.10) | copy-start | bytes 393220
  6.5 9.8 %copy-start.1 = (bf16[2,256]{1,0:T(2,128)(2,1)S(1)}, bf16[2,256]{1,0:T(2,128)(2,1)}, u32[]{:S(2)}) copy-start(bf16[2,256]{1,0:T(2,128)(2,1)} %param.9) | copy-start | bytes 3076
  6.5 68.8 %reduce-scatter.3.cloned.1.call-start = ((), (), s32[]{:S(2)}) async-start(), calls=%async_computation.4 | async-start | bytes 557056 | tf_op jit(solution)/shard_map/reduce_scatter | solution.py:77
  85.0 13.8 %all-to-all-start = ((bf16[16,16,2,256]{3,2,1,0:T(2,128)(2,1)}), bf16[16,16,2,256]{3,2,1,0:T(2,128)(2,1)S(1)}, u32[]{:S(2)}, u32[]{:S(2)}) async-start(bf16[16,16,2,256]{3,2,1,0:T(2,128)(2,1)} %stack.46), calls=%async_computation.1 | async-start | bytes 524288 | tf_op jit(solution)/shard_map/all_to_all | solution.py:82
  88.8 111.1 %reduce-scatter.5.cloned.1.call-start = ((), (), s32[]{:S(2)}) async-start(), calls=%async_computation.5 | async-start | bytes 557056 | tf_op jit(solution)/shard_map/reduce_scatter | solution.py:77
  99.1 11.4 %copy-start.2 = (bf16[2,256,256]{2,1,0:T(8,128)(2,1)S(1)}, bf16[2,256,256]{2,1,0:T(8,128)(2,1)}, u32[]{:S(2)}) copy-start(bf16[2,256,256]{2,1,0:T(8,128)(2,1)} %param.8) | copy-start | bytes 786436
  258.6 18.7 %copy-start.3 = (bf16[20,256]{1,0:T(8,128)(2,1)S(1)}, bf16[20,256]{1,0:T(8,128)(2,1)}, u32[]{:S(2)}) copy-start(bf16[20,256]{1,0:T(8,128)(2,1)} %param.11) | copy-start | bytes 30724
Sparse Core Ops, SparseCore 0:
  16.4 58.8 reduce-scatter.2
  145.5 54.3 reduce-scatter.4
